TPU v7x, 32 devices: a whole 2x2x4 slice. The times are simulated.
32 devices in a mesh: dp: 8 (over z, y), feat: 4 (over x, core).
Axes of the slice: x: 2, y: 2, z: 4, core: 2. Of those that a mesh axis runs over, the one named last changes fastest.
Arguments:
- observations: bfloat16 [1024, 128, 128], P('dp', 'feat'), may hold values from -1.5 to 1.5
- labels: int32 [1024, 128], P('dp'), may hold values 0 or 1
- tile_live: int32 [1024], P('dp'), may hold values from 1 to 128
- tile_group: int32 [1024], P('dp'), may hold values from 0 to 127, as said below
- position: float32 [128, 2048], P('dp', 'feat'), may hold values from -2.4 to 2.4
- momentum: float32 [128, 2048], P('dp', 'feat'), may hold values from -6 to 6
- gradient: float32 [128, 2048], P('dp', 'feat'), may hold values from -18 to 18
- prior_mean: float32 [2048], P('feat'), may hold values from -1.8 to 1.8
- prior_prec: float32 [128], P('feat'), may hold values from 0.25 to 4
- inv_mass: float32 [128], P('feat'), may hold values from 0.5 to 2
Outputs:
- new_position: float32 [128, 2048], P('dp', 'feat')
- new_momentum: float32 [128, 2048], P('dp', 'feat')
- new_gradient: float32 [128, 2048], P('dp', 'feat')
- energy: float32 [128, 16], P('dp')
Inputs may be any that keep to these rules, and one draw needn't show every extreme that they name: `tile_group`: group g belongs to owner g // 16. Among the 128 tiles of one device at most 32 have groups of any one owner, and one owner has exactly 32 tiles from every device. `tile_live`: the live slots of a tile come first.
All inputs are finite; a program needn't handle non-finite values. No bound on the sum of `labels` on one device may be relied on, other than what follows from the above.
Results may differ from a plain program's by a relative error of at most 0.0041.
Values may be sent and summed in bfloat16 or wider, within the bound.
A program may use at most 64 MiB of HBM per device.

v0:
```python
import jax
import jax.numpy as jnp
from jax import lax
from jax.sharding import PartitionSpec as P

step_size = 0.1


def likelihood(logits, labels, tile_live):
    row_count = logits.shape[2]
    live_rows = (jnp.arange(row_count, dtype=jnp.int32)[None, :] < tile_live[:, None])[:, None, :]
    targets = labels.astype(jnp.float32)[:, None, :]
    residual = jnp.where(live_rows, jax.nn.sigmoid(logits) - targets, 0.0).astype(jnp.bfloat16)
    neg_loglik = jnp.sum(
        jnp.where(live_rows, jax.nn.softplus(logits) - targets * logits, 0.0), axis=2
    )
    return (residual, neg_loglik)


def body(
    observations,
    labels,
    tile_live,
    tile_group,
    position,
    momentum,
    gradient,
    prior_mean,
    prior_prec,
    inv_mass,
):
    owners = lax.axis_size("dp")
    owner_index = lax.axis_index("dp")
    tile_count, quarter, row_count = observations.shape
    own_groups = position.shape[0]
    block_width = position.shape[1]
    chains = block_width // quarter
    slot_count = max(2, 2 * tile_count // owners)
    prior_full = jnp.repeat(prior_prec, chains)
    mass_full = jnp.repeat(inv_mass, chains)
    half_momentum = momentum - 0.5 * step_size * gradient
    moved_position = position + step_size * mass_full * half_momentum
    rounded = moved_position.astype(jnp.bfloat16)
    target = tile_group // own_groups
    tile_order = jnp.arange(tile_count, dtype=jnp.int32)
    earlier = (target[:, None] == target[None, :]) & (tile_order[None, :] < tile_order[:, None])
    slot_rank = jnp.sum(earlier.astype(jnp.int32), axis=1)
    slot_place = target * slot_count + slot_rank
    slot_tile = jnp.full((owners * slot_count,), -1, jnp.int32).at[slot_place].set(tile_order)
    filled = slot_tile >= 0
    safe_tile = jnp.maximum(slot_tile, 0)
    requests = jnp.where(filled, tile_group[safe_tile], -1).reshape(owners, slot_count)
    group_order = jnp.arange(own_groups, dtype=jnp.int32)
    asked_groups = lax.all_to_all(requests, "dp", split_axis=0, concat_axis=0, tiled=True)
    local_group = asked_groups - owner_index * own_groups
    selector = (local_group[:, :, None] == group_order[None, None, :]).astype(jnp.bfloat16)
    picked = jnp.einsum(
        "nkg,gw->nkw", selector, rounded, preferred_element_type=jnp.float32
    ).astype(jnp.bfloat16)
    fetched = lax.all_to_all(picked, "dp", split_axis=0, concat_axis=0, tiled=True)
    tile_blocks = fetched.reshape(owners * slot_count, block_width)[slot_place]
    tile_coeffs = tile_blocks.reshape(tile_count, quarter, chains)
    partial_logits = jnp.einsum(
        "tfc,tfr->tcr", tile_coeffs, observations, preferred_element_type=jnp.float32
    )
    logit_share = lax.psum_scatter(partial_logits, "feat", scatter_dimension=0, tiled=True)
    share_count = logit_share.shape[0]
    share_start = lax.axis_index("feat") * share_count
    share_labels = lax.dynamic_slice_in_dim(labels, share_start, share_count, 0)
    share_live = lax.dynamic_slice_in_dim(tile_live, share_start, share_count, 0)
    residual_share, loglik_share = likelihood(logit_share, share_labels, share_live)
    residual = lax.all_gather(residual_share, "feat", axis=0, tiled=True)
    neg_loglik = lax.dynamic_update_slice_in_dim(
        jnp.zeros((tile_count, chains), jnp.float32), loglik_share, share_start, 0
    )
    partial_grad = jnp.einsum(
        "tfr,tcr->tfc", observations, residual, preferred_element_type=jnp.float32
    ).reshape(tile_count, block_width)
    send_grad = jnp.where(filled[:, None], partial_grad[safe_tile], 0.0).reshape(
        owners, slot_count, block_width
    )
    send_loglik = jnp.where(filled[:, None], neg_loglik[safe_tile], 0.0).reshape(
        owners, slot_count, chains
    )
    got_grad, got_loglik = (
        lax.all_to_all(send_grad, "dp", split_axis=0, concat_axis=0, tiled=True),
        lax.all_to_all(send_loglik, "dp", split_axis=0, concat_axis=0, tiled=True),
    )
    local_slot = asked_groups.reshape(-1) - owner_index * own_groups
    collector = (group_order[:, None] == local_slot[None, :]).astype(jnp.float32)
    likelihood_grad = jnp.dot(
        collector,
        got_grad.reshape(-1, block_width),
        precision=lax.Precision.HIGHEST,
        preferred_element_type=jnp.float32,
    )
    group_loglik = jnp.dot(
        collector,
        got_loglik.reshape(-1, chains),
        precision=lax.Precision.HIGHEST,
        preferred_element_type=jnp.float32,
    )
    offset = moved_position - prior_mean
    new_gradient = likelihood_grad + prior_full * offset
    new_momentum = half_momentum - 0.5 * step_size * new_gradient
    quadratic = 0.5 * (prior_full * offset * offset + mass_full * new_momentum * new_momentum)
    quadratic = jnp.sum(quadratic.reshape(own_groups, quarter, chains), axis=1)
    summed = quadratic + group_loglik
    energy = lax.psum(summed, "feat")
    return (moved_position, new_momentum, new_gradient, energy)


def solution(mesh):
    placed = (
        P("dp", "feat", None),
        P("dp", None),
        P("dp"),
        P("dp"),
        P("dp", "feat"),
        P("dp", "feat"),
        P("dp", "feat"),
        P("feat"),
        P("feat"),
        P("feat"),
    )
    return jax.shard_map(
        body,
        mesh=mesh,
        in_specs=placed,
        out_specs=(P("dp", "feat"), P("dp", "feat"), P("dp", "feat"), P("dp", None)),
        check_vma=False,
    )
```

profile of v0, /device:TPU:0, one launch (start us, length us, event | category | flops | bytes accessed | tf_op | source)
XLA Modules:
  0.0 121.5 jit_solution(3610660603039455534)
XLA Ops:
  7.2 0.8 and_select_fusion
  8.6 1.0 scatter_custom_fusion
  9.7 1.9 %gather_fusion = s32[256]{0:T(256)S(1)} fusion(s32[128]{0:T(128)S(1)} %copy-done.1, s32[1024]{0:T(1024)S(1)} %pad_clamp_fusion.1), kind=kCustom, calls=%fused_computation | custom fusion | bytes 3072 | tf_op jit(solution)/shard_map/gather | solution.py:52
  12.2 7.3 %all-to-all-start = ((s32[8,1,32]{2,1,0:T(1,128)}), s32[8,1,32]{2,1,0:T(1,128)S(1)}, u32[]{:S(2)}, u32[]{:S(2)}) async-start(s32[8,1,32]{2,1,0:T(1,128)} %all_to_all.15), calls=%async_computation | async-start | bytes 8192 | tf_op jit(solution)/shard_map/all_to_all | solution.py:54
  19.8 6.2 %all-to-all-done = s32[8,1,32]{2,1,0:T(1,128)S(1)} async-done(((s32[8,1,32]{2,1,0:T(1,128)}), s32[8,1,32]{2,1,0:T(1,128)S(1)}, u32[]{:S(2)}, u32[]{:S(2)}) %all-to-all-start) | async-done | bytes 1056 | tf_op jit(solution)/shard_map/all_to_all | solution.py:54
  27.1 1.0 convolution_convert_fusion
  28.1 3.4 %all-to-all-start.1 = ((bf16[8,32,512]{2,1,0:T(8,128)(2,1)}), bf16[8,32,512]{2,1,0:T(8,128)(2,1)S(1)}, u32[]{:S(2)}, u32[]{:S(2)}) async-start(bf16[8,32,512]{2,1,0:T(8,128)(2,1)} %convolution_convert_fusion), calls=%async_computation.1 | async-start | bytes 524288 | tf_op jit(solution)/shard_map/all_to_all | solution.py:60
  31.6 8.1 %all-to-all-done.1 = bf16[8,32,512]{2,1,0:T(8,128)(2,1)S(1)} async-done(((bf16[8,32,512]{2,1,0:T(8,128)(2,1)}), bf16[8,32,512]{2,1,0:T(8,128)(2,1)S(1)}, u32[]{:S(2)}, u32[]{:S(2)}) %all-to-all-start.1) | async-done | bytes 262176 | tf_op jit(solution)/shard_map/all_to_all | solution.py:60
  39.7 0.8 gather_fusion.1
  41.1 1.4 %fusion.15 = f32[128,16,128]{2,1,0:T(8,128)} fusion(bf16[128,32,16]{1,2,0:T(8,128)(2,1)S(1)} %copy.31, bf16[128,32,128]{2,1,0:T(8,128)(2,1)S(1)} %copy-done), kind=kOutput, calls=%fused_computation.52 | convolution fusion | flops 16777216 | bytes 2228224 | tf_op jit(solution)/shard_map/tfc,tfr->tcr/dot_general | solution.py:63
  43.4 0.7 dynamic-slice_convert_fusion
  44.2 21.8 %reduce-scatter.2.cloned.1.call-done = f32[32,16,128]{2,1,0:T(8,128)} async-done(((f32[128,16,128]{2,1,0:T(8,128)}), f32[32,16,128]{2,1,0:T(8,128)}) %reduce-scatter.2.cloned.1.call-update) | async-done | bytes 262160 | tf_op jit(solution)/shard_map/reduce_scatter | solution.py:66
  66.0 1.3 %fusion.2 = (f32[32,16]{1,0:T(8,128)S(1)}, bf16[32,16,128]{2,1,0:T(8,128)(2,1)S(1)}) fusion(f32[32,16,128]{2,1,0:T(8,128)} %reduce-scatter.2.cloned.1.call-done, f32[32,128]{1,0:T(8,128)S(1)} %dynamic-slice_convert_fusion, pred[32,128]{1,0:T(8,128)(4,1)S(1)} %iota_compare_fusion.3), kind=kLoop, calls=%fused_computation.12 | loop fusion | flops 1048064 | bytes 415744 | tf_op jit(solution)/shard_map/reduce_sum | solution.py:14
  67.2 6.6 %all_gather.3 = bf16[128,16,128]{2,1,0:T(8,128)(2,1)S(1)} all-gather(bf16[32,16,128]{2,1,0:T(8,128)(2,1)S(1)} %get-tuple-element.11), channel_id=1, replica_groups=mesh['dp'=8,'feat'=4] {'feat'}, dimensions={0}, use_global_device_ids=true | all-gather | bytes 655360 | tf_op jit(solution)/shard_map/all_gather | solution.py:72
  75.1 1.0 gather_fusion.2
  76.1 0.7 gather_fusion.3
  77.0 0.7 reshape.155
  77.7 5.5 %all-to-all-start.3 = ((f32[8,1,512]{2,1,0:T(1,128)}), f32[8,1,512]{2,1,0:T(1,128)S(1)}, u32[]{:S(2)}, u32[]{:S(2)}) async-start(f32[8,1,512]{2,1,0:T(1,128)} %reshape.155), calls=%async_computation.4 | async-start | bytes 32768 | tf_op jit(solution)/shard_map/all_to_all | solution.py:87
  83.2 0.9 broadcast_select_fusion
  84.1 5.7 %all-to-all-done.3 = f32[8,1,512]{2,1,0:T(1,128)S(1)} async-done(((f32[8,1,512]{2,1,0:T(1,128)}), f32[8,1,512]{2,1,0:T(1,128)S(1)}, u32[]{:S(2)}, u32[]{:S(2)}) %all-to-all-start.3) | async-done | bytes 16416 | tf_op jit(solution)/shard_map/all_to_all | solution.py:87
  89.8 3.5 %all-to-all-start.2 = ((f32[8,32,512]{2,1,0:T(8,128)}), f32[8,32,512]{2,1,0:T(8,128)S(1)}, u32[]{:S(2)}, u32[]{:S(2)}) async-start(f32[8,32,512]{2,1,0:T(8,128)} %broadcast_select_fusion), calls=%async_computation.3 | async-start | bytes 1048576 | tf_op jit(solution)/shard_map/all_to_all | solution.py:86
  94.9 12.2 %all-to-all-done.2 = f32[8,32,512]{2,1,0:T(8,128)S(1)} async-done(((f32[8,32,512]{2,1,0:T(8,128)}), f32[8,32,512]{2,1,0:T(8,128)S(1)}, u32[]{:S(2)}, u32[]{:S(2)}) %all-to-all-start.2) | async-done | bytes 524320 | tf_op jit(solution)/shard_map/all_to_all | solution.py:86
  107.1 0.9 fusion.5
  108.3 6.3 %psum.7 = f32[16,16]{1,0:T(8,128)} all-reduce(f32[16,16]{1,0:T(8,128)S(1)} %convolution_add_fusion.1), channel_id=1, replica_groups=mesh['dp'=8,'feat'=4] {'feat'}, use_global_device_ids=true, to_apply=%region_5.6 | all-reduce | flops 256 | bytes 2048 | tf_op jit(solution)/shard_map/psum | solution.py:109
  (59 shorter events, 7.6 us)
Async XLA Ops:
  7.2 34.0 %copy-start = (bf16[128,32,128]{2,1,0:T(8,128)(2,1)S(1)}, bf16[128,32,128]{2,1,0:T(8,128)(2,1)}, u32[]{:S(2)}) copy-start(bf16[128,32,128]{2,1,0:T(8,128)(2,1)} %param.10) | copy-start | bytes 3145732
  7.9 0.7 copy-start.1
  9.6 9.9 %copy-start.7 = (f32[32]{0:T(128)S(1)}, f32[32]{0:T(128)}, u32[]{:S(2)}) copy-start(f32[32]{0:T(128)} %param.19) | copy-start | bytes 388
  9.6 10.1 %copy-start.4 = (f32[16,512]{1,0:T(8,128)S(1)}, f32[16,512]{1,0:T(8,128)}, u32[]{:S(2)}) copy-start(f32[16,512]{1,0:T(8,128)} %param.16) | copy-start | bytes 98308
  9.6 10.1 %copy-start.5 = (f32[16,512]{1,0:T(8,128)S(1)}, f32[16,512]{1,0:T(8,128)}, u32[]{:S(2)}) copy-start(f32[16,512]{1,0:T(8,128)} %param.14) | copy-start | bytes 98308
  11.5 8.2 %copy-start.3 = (f32[16,512]{1,0:T(8,128)S(1)}, f32[16,512]{1,0:T(8,128)}, u32[]{:S(2)}) copy-start(f32[16,512]{1,0:T(8,128)} %param.15) | copy-start | bytes 98308
  12.2 13.7 %all-to-all-start = ((s32[8,1,32]{2,1,0:T(1,128)}), s32[8,1,32]{2,1,0:T(1,128)S(1)}, u32[]{:S(2)}, u32[]{:S(2)}) async-start(s32[8,1,32]{2,1,0:T(1,128)} %all_to_all.15), calls=%async_computation | async-start | bytes 8192 | tf_op jit(solution)/shard_map/all_to_all | solution.py:54
  19.8 87.3 %copy-start.2 = (f32[16,512]{1,0:T(8,128)}, f32[16,512]{1,0:T(8,128)S(1)}, u32[]{:S(2)}) copy-start(f32[16,512]{1,0:T(8,128)S(1)} %multiply_add_fusion) | copy-start | bytes 98308
  28.1 11.6 %all-to-all-start.1 = ((bf16[8,32,512]{2,1,0:T(8,128)(2,1)}), bf16[8,32,512]{2,1,0:T(8,128)(2,1)S(1)}, u32[]{:S(2)}, u32[]{:S(2)}) async-start(bf16[8,32,512]{2,1,0:T(8,128)(2,1)} %convolution_convert_fusion), calls=%async_computation.1 | async-start | bytes 524288 | tf_op jit(solution)/shard_map/all_to_all | solution.py:60
  31.5 34.5 %reduce-scatter.2.cloned.1.call-start = ((), (), s32[]{:S(2)}) async-start(), calls=%async_computation.5 | async-start | bytes 1310720 | tf_op jit(solution)/shard_map/reduce_scatter | solution.py:66
  42.6 0.7 copy-start.9
  77.7 12.1 %all-to-all-start.3 = ((f32[8,1,512]{2,1,0:T(1,128)}), f32[8,1,512]{2,1,0:T(1,128)S(1)}, u32[]{:S(2)}, u32[]{:S(2)}) async-start(f32[8,1,512]{2,1,0:T(1,128)} %reshape.155), calls=%async_computation.4 | async-start | bytes 32768 | tf_op jit(solution)/shard_map/all_to_all | solution.py:87
  84.1 9.2 %copy-start.8 = (f32[32]{0:T(128)S(1)}, f32[32]{0:T(128)}, u32[]{:S(2)}) copy-start(f32[32]{0:T(128)} %param.18) | copy-start | bytes 388
  89.8 17.3 %all-to-all-start.2 = ((f32[8,32,512]{2,1,0:T(8,128)}), f32[8,32,512]{2,1,0:T(8,128)S(1)}, u32[]{:S(2)}, u32[]{:S(2)}) async-start(f32[8,32,512]{2,1,0:T(8,128)} %broadcast_select_fusion), calls=%async_computation.3 | async-start | bytes 1048576 | tf_op jit(solution)/shard_map/all_to_all | solution.py:86
  94.8 12.3 %copy-start.6 = (f32[512]{0:T(512)S(1)}, f32[512]{0:T(512)}, u32[]{:S(2)}) copy-start(f32[512]{0:T(512)} %param.17) | copy-start | bytes 6148
Sparse Core Ops, SparseCore 0:
  42.7 23.2 reduce-scatter.1
where the time goes:
time: 122 us; the launch traced here: 121 us
  waiting for transfers between devices  54 us (44%)
  starting transfers between devices  19.8 us (16%)
  between operations  14.3 us (12%)
  blocking collectives  12.9 us (11%)
  local copies, waits for them, and re-layouts  11.1 us (9%)
  other arithmetic  5.32 us (4%)
  matrix products  4.04 us (3%)
    reduce_scatter x1, waiting for transfers between devices, body(): lax.psum_scatter(partial_logits, 'feat', scatter_dimension=0, tiled=True)  21.8 us
    all_to_all x1, waiting for transfers between devices, body(): lax.all_to_all(send_grad, 'dp', split_axis=0, concat_axis=0, tiled=True)  12.2 us
    all_to_all x1, waiting for transfers between devices, body(): lax.all_to_all(picked, 'dp', split_axis=0, concat_axis=0, tiled=True)  8.1 us
    all_to_all x1, starting transfers between devices, body(): lax.all_to_all(requests, 'dp', split_axis=0, concat_axis=0, tiled=True)  7.31 us
    all_gather x1, blocking collectives, body(): residual = lax.all_gather(residual_share, 'feat', axis=0, tiled=True)  6.59 us
    psum x1, blocking collectives, body(): energy = lax.psum(summed, 'feat')  6.34 us
    all_to_all x1, waiting for transfers between devices, body(): lax.all_to_all(requests, 'dp', split_axis=0, concat_axis=0, tiled=True)  6.19 us
    all_to_all x1, waiting for transfers between devices, body(): lax.all_to_all(send_loglik, 'dp', split_axis=0, concat_axis=0, tiled=True)  5.68 us
  transfers between devices with their start and end apart: 5, of which 5 were waited for; matrix products, arithmetic and copies ran while one was open for 3% of the time, Pallas kernels for 0%

commit v1 on v0

v1 whole, which is shorter than its diff:
```python
import functools
import jax
import jax.numpy as jnp
from jax import lax
from jax.experimental import pallas as pl
from jax.experimental.pallas import tpu as pltpu
from jax.sharding import PartitionSpec as P

step_size = 0.1
LANES = 128
CHUNKS = 4
MESH = pl.DeviceIdType.MESH
BF16 = jnp.bfloat16
F32 = jnp.float32


def iota(shape, dim):
    return lax.broadcasted_iota(jnp.int32, shape, dim)


def split(x):
    hi = x.astype(BF16)
    return hi, (x - hi.astype(F32)).astype(BF16)


def nt_dot(a, b):
    return lax.dot_general(a, b, (((1,), (1,)), ((), ())), preferred_element_type=F32)


def kernel(
    n, nf, chains, quarter,
    obs_hbm, lab_ref, grp_ref, pos_ref, mom_ref, grad_ref, par_ref,
    newpos_ref, newmom_ref, newgrad_ref, energy_ref,
    obs, perm, wsrc, wall, half_ref, lhs, mine, pair_send, pair_recv,
    far_send, far_recv, res_own, res_recv, nll_ref, dmat, gsend, grecv, esend, erecv,
    obs_sem, w_ssem, w_rsem, p_ssem, p_rsem, f_ssem, f_rsem, r_ssem, r_rsem,
    g_ssem, g_rsem, e_ssem, e_rsem,
):
    me = lax.axis_index("dp")
    feat = lax.axis_index("feat")
    tiles = lab_ref.shape[0]
    own, width = pos_ref.shape
    pack = LANES // quarter
    quads = tiles // pack
    qrows = pack * chains
    half_quads = quads // 2
    chunk_quads = half_quads // CHUNKS
    chunk_tiles = chunk_quads * pack
    crows = chunk_quads * qrows
    groups = n * own
    bit = feat % 2
    near = feat + 1 - 2 * bit
    far = (feat + nf // 2) % nf

    fetch = pltpu.make_async_copy(obs_hbm, obs, obs_sem)
    fetch.start()
    barrier = pltpu.get_barrier_semaphore()

    def greet(i, carry):
        pl.semaphore_signal(barrier, inc=1, device_id={"dp": (me + i) % n}, device_id_type=MESH)
        return carry

    lax.fori_loop(1, n, greet, 0)
    for i in range(1, nf):
        pl.semaphore_signal(barrier, inc=1, device_id={"feat": (feat + i) % nf}, device_id_type=MESH)

    r, c = iota((width, width), 0), iota((width, width), 1)
    perm[...] = jnp.where(
        (r % chains == c // quarter) & (r // chains == c % quarter), 1.0, 0.0
    ).astype(BF16)
    half = mom_ref[...] - 0.5 * step_size * grad_ref[...]
    half_ref[...] = half
    moved = pos_ref[...] + step_size * par_ref[2:3, :] * half
    newpos_ref[...] = moved
    coeff = jnp.dot(moved.astype(BF16), perm[...], preferred_element_type=F32).astype(BF16)
    wsrc[...] = coeff
    own_rows = pl.ds(pl.multiple_of(me * own, own), own)
    wall[own_rows, :] = coeff
    pl.semaphore_wait(barrier, n - 1 + nf - 1)

    def w_copy(i):
        to = (me + i) % n
        return pltpu.make_async_remote_copy(
            src_ref=wsrc, dst_ref=wall.at[own_rows], send_sem=w_ssem.at[i],
            recv_sem=w_rsem.at[i], device_id={"dp": to}, device_id_type=MESH,
        )

    def start_w(i, carry):
        w_copy(i).start()
        return carry

    lax.fori_loop(1, n, start_w, 0)
    seg_groups = min(groups, LANES)
    hot = (iota((groups, tiles), 0) == grp_ref[...]).astype(F32).astype(BF16)

    def wait_w(i, carry):
        w_copy(i).wait()
        return carry

    lax.fori_loop(1, n, wait_w, 0)
    picked = lax.dot_general(
        hot, wall[...], (((0,), (0,)), ((), ())), preferred_element_type=F32
    )
    row_t, lane_t = iota((tiles, LANES), 0), iota((tiles, LANES), 1)
    place = row_t % pack
    keep = lane_t // quarter == place
    for m in range(width // LANES):
        x = picked[:, m * LANES:(m + 1) * LANES]
        turned = [x] + [pltpu.roll(x, s * quarter, 1) for s in range(1, pack)]
        for j in range(pack):
            y = turned[0]
            for s in range(1, pack):
                y = jnp.where((place + pack - j) % pack == s, turned[s], y)
            lhs[pl.ds(m * pack + j, tiles, stride=chains), :] = jnp.where(keep, y, 0.0)
    fetch.wait()

    def logits(first_quad, dst, base):
        for i in range(chunk_quads):
            q = first_quad + i
            a = lhs[pl.ds(pl.multiple_of(q * qrows, qrows), qrows), :].astype(BF16)
            dst[pl.ds(pl.multiple_of(base + i * qrows, qrows), qrows), :] = jnp.dot(
                a, obs[q], preferred_element_type=F32
            )

    def rows(k):
        return pl.ds(pl.multiple_of(k * crows, crows), crows)

    def pair_copy(k):
        return pltpu.make_async_remote_copy(
            src_ref=pair_send.at[rows(k)], dst_ref=pair_recv.at[rows(k)],
            send_sem=p_ssem.at[k], recv_sem=p_rsem.at[k],
            device_id={"feat": near}, device_id_type=MESH,
        )

    def far_copy(k):
        return pltpu.make_async_remote_copy(
            src_ref=far_send.at[rows(k)], dst_ref=far_recv.at[rows(k)],
            send_sem=f_ssem.at[k], recv_sem=f_rsem.at[k],
            device_id={"feat": far}, device_id_type=MESH,
        )

    def res_copy(k):
        return pltpu.make_async_remote_copy(
            src_ref=res_own.at[rows(k)], dst_ref=res_recv.at[rows(k)],
            send_sem=r_ssem.at[k], recv_sem=r_rsem.at[k],
            device_id={"feat": near}, device_id_type=MESH,
        )

    def stage_a(k, carry):
        logits((1 - bit) * half_quads + k * chunk_quads, pair_send, k * crows)
        pair_copy(k).start()
        logits(bit * half_quads + k * chunk_quads, mine, k * crows)
        return carry

    lax.fori_loop(0, CHUNKS, stage_a, 0)

    def stage_b(k, carry):
        pair_copy(k).wait()
        total = mine[rows(k), :] + pair_recv[rows(k), :]
        mine[rows(k), :] = total
        far_send[rows(k), :] = total.astype(BF16)
        far_copy(k).start()
        return carry

    lax.fori_loop(0, CHUNKS, stage_b, 0)

    nll_ref[...] = jnp.zeros_like(nll_ref)
    diag = iota((qrows, LANES), 0) // chains == iota((qrows, LANES), 1) // quarter

    def grads(first_quad, src, k):
        for i in range(chunk_quads):
            q = first_quad + i
            a = src[pl.ds(pl.multiple_of(k * crows + i * qrows, qrows), qrows), :]
            g = jnp.where(diag, nt_dot(a, obs[q]), 0.0)
            for j in range(pack):
                dmat[pl.ds(q * pack + j, chains, stride=tiles), :] = g[j * chains:(j + 1) * chains]

    def stage_c(k, carry):
        far_copy(k).wait()
        z = mine[rows(k), :] + far_recv[rows(k), :].astype(F32)
        first = pl.multiple_of((bit * half_quads + k * chunk_quads) * pack, chunk_tiles)
        lab = lab_ref[pl.ds(first, chunk_tiles), :]
        lab = jnp.broadcast_to(lab[:, None, :], (chunk_tiles, chains, LANES)).reshape(crows, LANES)
        live = lab >= 0.0
        e = jnp.exp(-jnp.abs(z))
        inv = 1.0 / (1.0 + e)
        sig = jnp.where(z >= 0.0, inv, e * inv)
        res_own[rows(k), :] = jnp.where(live, sig - lab, 0.0).astype(BF16)
        res_copy(k).start()
        v = jnp.where(live, jnp.maximum(z, 0.0) + jnp.log1p(e) - lab * z, 0.0)
        s = jnp.sum(v, axis=1, keepdims=True) * (2.0 / nf)
        at = iota((crows, LANES), 0) % chains == iota((crows, LANES), 1)
        s = jnp.where(at, s, 0.0).reshape(chunk_tiles, chains, LANES)
        nll_ref[pl.ds(first, chunk_tiles), :] = jnp.sum(s, axis=1)
        grads(bit * half_quads + k * chunk_quads, res_own, k)
        return carry

    lax.fori_loop(0, CHUNKS, stage_c, 0)

    def stage_d(k, carry):
        res_copy(k).wait()
        grads((1 - bit) * half_quads + k * chunk_quads, res_recv, k)
        return carry

    lax.fori_loop(0, CHUNKS, stage_d, 0)

    lane_g = iota((seg_groups, LANES), 1) // quarter

    def segment(gc, carry):
        base = gc * seg_groups
        out = pl.ds(pl.multiple_of(base, seg_groups), seg_groups)
        oh = (iota((seg_groups, tiles), 0) + base == grp_ref[...]).astype(F32).astype(BF16)
        oh = jnp.concatenate([oh, oh], axis=1)

        def stacked(d):
            return jnp.concatenate(split(d), axis=0)

        for m in range(width // LANES):
            packed = None
            for j in range(0, pack, 2):
                at = (m * pack + j) * tiles
                rhs = jnp.concatenate(
                    [stacked(dmat[at:at + tiles]), stacked(dmat[at + tiles:at + 2 * tiles])], axis=1
                )
                both = jnp.dot(oh, rhs, preferred_element_type=F32)
                for h in range(2):
                    s = both[:, h * LANES:(h + 1) * LANES]
                    shift = LANES // 2
                    while shift >= quarter:
                        s = s + pltpu.roll(s, shift, 1)
                        shift //= 2
                    packed = s if packed is None else jnp.where(lane_g == j + h, s, packed)
            gsend[out, m * LANES:(m + 1) * LANES] = packed.astype(BF16)
        hi, lo = split(jnp.dot(oh, stacked(nll_ref[...]), preferred_element_type=F32))
        gsend[out, width:width + LANES] = (
            hi.astype(F32) + pltpu.roll(lo.astype(F32), chains, 1)
        ).astype(BF16)
        return carry

    lax.fori_loop(0, groups // seg_groups, segment, 0)

    def g_copy(i):
        to = (me + i) % n
        return pltpu.make_async_remote_copy(
            src_ref=gsend.at[pl.ds(pl.multiple_of(to * own, own), own)],
            dst_ref=grecv.at[me], send_sem=g_ssem.at[i], recv_sem=g_rsem.at[i],
            device_id={"dp": to}, device_id_type=MESH,
        )

    def start_g(i, carry):
        g_copy(i).start()
        return carry

    lax.fori_loop(1, n, start_g, 0)
    grecv[me] = gsend[own_rows, :]

    def wait_g(i, carry):
        g_copy(i).wait()
        return carry

    lax.fori_loop(1, n, wait_g, 0)

    def add_g(i, total):
        return total + grecv[i].astype(F32)

    total = lax.fori_loop(0, n, add_g, jnp.zeros((own, width + LANES), F32))
    parts = jnp.concatenate(split(total[:, :width]), axis=0)
    natural = nt_dot(parts, perm[...])
    lik = natural[:own] + natural[own:]
    mean, prec, mass = par_ref[0:1, :], par_ref[1:2, :], par_ref[2:3, :]
    offset = newpos_ref[...] - mean
    new_gradient = lik + prec * offset
    new_momentum = half_ref[...] - 0.5 * step_size * new_gradient
    newgrad_ref[...] = new_gradient
    newmom_ref[...] = new_momentum
    quad = 0.5 * (prec * offset * offset + mass * new_momentum * new_momentum)
    q = quad[:, :LANES]
    for m in range(1, width // LANES):
        q = q + quad[:, m * LANES:(m + 1) * LANES]
    shift = LANES // 2
    while shift >= chains:
        q = q + pltpu.roll(q, shift, 1)
        shift //= 2
    loss = total[:, width:]
    loss = loss + pltpu.roll(loss, LANES - chains, 1)
    esend[...] = q + loss

    def e_copy(i):
        return pltpu.make_async_remote_copy(
            src_ref=esend, dst_ref=erecv.at[feat], send_sem=e_ssem.at[i],
            recv_sem=e_rsem.at[i], device_id={"feat": (feat + i) % nf}, device_id_type=MESH,
        )

    for i in range(1, nf):
        e_copy(i).start()
    erecv[feat] = esend[...]
    for i in range(1, nf):
        e_copy(i).wait()
    e = erecv[0]
    for i in range(1, nf):
        e = e + erecv[i]
    energy_ref[...] = e[:, :chains]


def body(observations, labels, tile_live, tile_group, position, momentum, gradient, prior_mean, prior_prec, inv_mass):
    n, nf = lax.axis_size("dp"), lax.axis_size("feat")
    tiles, quarter, row_count = observations.shape
    own, width = position.shape
    chains = width // quarter
    pack = LANES // quarter
    alive = jnp.arange(row_count, dtype=jnp.int32)[None, :] < tile_live[:, None]
    marked = jnp.where(alive, labels, -1).astype(F32)
    par = jnp.stack([prior_mean, jnp.repeat(prior_prec, chains), jnp.repeat(inv_mass, chains)])
    half_rows = tiles * chains // 2
    vmem = pl.BlockSpec(memory_space=pltpu.VMEM)
    dma = pltpu.SemaphoreType.DMA
    block = jax.ShapeDtypeStruct((own, width), F32)
    return tuple(pl.pallas_call(
        functools.partial(kernel, n, nf, chains, quarter),
        out_shape=(block, block, block, jax.ShapeDtypeStruct((own, chains), F32)),
        in_specs=[pl.BlockSpec(memory_space=pl.ANY)] + [vmem] * 6,
        out_specs=(vmem,) * 4,
        scratch_shapes=[
            pltpu.VMEM((tiles // pack, LANES, row_count), BF16),
            pltpu.VMEM((width, width), BF16),
            pltpu.VMEM((own, width), BF16),
            pltpu.VMEM((n * own, width), BF16),
            pltpu.VMEM((own, width), F32),
            pltpu.VMEM((tiles * chains, LANES), F32),
            pltpu.VMEM((half_rows, row_count), F32),
            pltpu.VMEM((half_rows, row_count), F32),
            pltpu.VMEM((half_rows, row_count), F32),
            pltpu.VMEM((half_rows, row_count), BF16),
            pltpu.VMEM((half_rows, row_count), BF16),
            pltpu.VMEM((half_rows, row_count), BF16),
            pltpu.VMEM((half_rows, row_count), BF16),
            pltpu.VMEM((tiles, LANES), F32),
            pltpu.VMEM((chains * tiles, LANES), F32),
            pltpu.VMEM((n * own, width + LANES), BF16),
            pltpu.VMEM((n, own, width + LANES), BF16),
            pltpu.VMEM((own, LANES), F32),
            pltpu.VMEM((nf, own, LANES), F32),
            dma,
            dma((n,)), dma((n,)),
            dma((CHUNKS,)), dma((CHUNKS,)),
            dma((CHUNKS,)), dma((CHUNKS,)),
            dma((CHUNKS,)), dma((CHUNKS,)),
            dma((n,)), dma((n,)),
            dma((nf,)), dma((nf,)),
        ],
        compiler_params=pltpu.CompilerParams(collective_id=0, has_side_effects=True),
    )(
        observations.reshape(tiles // pack, LANES, row_count),
        marked,
        tile_group.reshape(1, tiles),
        position, momentum, gradient, par,
    ))


def solution(mesh):
    placed = (
        P("dp", "feat", None),
        P("dp", None),
        P("dp"),
        P("dp"),
        P("dp", "feat"),
        P("dp", "feat"),
        P("dp", "feat"),
        P("feat"),
        P("feat"),
        P("feat"),
    )
    return jax.shard_map(
        body,
        mesh=mesh,
        in_specs=placed,
        out_specs=(P("dp", "feat"), P("dp", "feat"), P("dp", "feat"), P("dp", None)),
        check_vma=False,
    )
```

time: 122 us -> 41.3 us (0.34)
  waiting for transfers between devices: 54 us -> 0 us
  Pallas kernels: 0 us -> 33.1 us
  starting transfers between devices: 19.8 us -> 0 us
  between operations: 14.3 us -> 0.66 us
  blocking collectives: 12.9 us -> 0 us
  local copies, waits for them, and re-layouts: 11.1 us -> 5.76 us
  matrix products: 4.04 us -> 0 us
  other arithmetic: 5.32 us -> 1.32 us
    pallas_call x0 -> x1, Pallas kernels: none -> 33.1 us  [body(): pl.pallas_call(functools.partial(kernel, n, nf, chains, quarter), out_sha...]
    all_to_all x4 -> x0, waiting for transfers between devices: 32.1 us -> none  [the longest x1 12.2 us: body(): lax.all_to_all(send_grad, 'dp', split_axis=0, concat_axis=0, tiled=True)]
    reduce_scatter x1 -> x0, waiting for transfers between devices: 21.8 us -> none  [body(): lax.psum_scatter(partial_logits, 'feat', scatter_dimension=0, tiled=True)]
    all_to_all x4 -> x0, starting transfers between devices: 19.7 us -> none  [the longest x1 7.31 us: body(): lax.all_to_all(requests, 'dp', split_axis=0, concat_axis=0, tiled=True)]
    all_gather x1 -> x0, blocking collectives: 6.59 us -> none  [body(): residual = lax.all_gather(residual_share, 'feat', axis=0, tiled=True)]
    psum x1 -> x0, blocking collectives: 6.34 us -> none  [body(): energy = lax.psum(summed, 'feat')]
    gather x6 -> x0, local copies, waits for them, and re-layouts: 4.62 us -> none  [the longest x1 1.87 us: body(): tile_group[safe_tile]]
    dot_general x5 -> x0, matrix products: 4.04 us -> none  [the longest x1 1.39 us: body(): jnp.einsum('tfc,tfr->tcr', tile_coeffs, observations, preferred_element_t...]
  transfers between devices with their start and end apart: 5 -> 0, of which waited for: 5 -> 0; matrix products, arithmetic and copies ran while one was open for 3% -> 0% of each run, Pallas kernels for 0% -> 0%
where the time goes in v1:
time: 41.3 us; the launch traced here: 40.8 us
  Pallas kernels  33.1 us (80%)
  local copies, waits for them, and re-layouts  5.76 us (14%)
  other arithmetic  1.32 us (3%)
  between operations  0.66 us (2%)
    pallas_call x1, Pallas kernels, body(): pl.pallas_call(functools.partial(kernel, n, nf, chains, quarter), out_sha...  33.1 us
    unnamed x16, local copies, waits for them, and re-layouts  4.11 us

profile of v1, /device:TPU:0, one launch (start us, length us, event | category | flops | bytes accessed | tf_op | source)
XLA Modules:
  0.0 40.8 jit_solution(622456847626163707)
XLA Ops:
  0.6 0.0 copy-start
  0.6 0.8 %broadcast_in_dim.13 = f32[32,16]{1,0:T(8,128)S(1)} broadcast(f32[32]{0:T(128)} %param.18), dimensions={0} | broadcast | bytes 2176 | tf_op jit(solution)/shard_map/broadcast_in_dim | solution.py:313
  1.4 0.1 stack_reshape.6
  1.5 0.7 %broadcast_in_dim.14 = f32[32,16]{1,0:T(8,128)S(1)} broadcast(f32[32]{0:T(128)} %param.19), dimensions={0} | broadcast | bytes 2176 | tf_op jit(solution)/shard_map/broadcast_in_dim | solution.py:313
  2.2 0.0 copy-start.4
  2.2 0.1 stack_reshape.7
  2.3 0.6 %copy-done.4 = f32[512]{0:T(512)S(1)} copy-done((f32[512]{0:T(512)S(1)}, f32[512]{0:T(512)}, u32[]{:S(2)}) %copy-start.4) | copy-done | bytes 2072
  2.9 0.0 copy-start.5
  2.9 0.6 %pad_maximum_fusion.par_ref = f32[3,512]{1,0:T(4,128)} fusion(f32[1,512]{1,0:T(1,128)S(1)} %stack_reshape.7, f32[1,512]{1,0:T(1,128)S(1)} %stack_reshape.6, f32[1,512]{1,0:T(1,128)S(1)} %bitcast.4), kind=kLoop, calls=%fused_computation.2 | loop fusion | flops 3072 | bytes 12288 | tf_op jit(solution)/shard_map/stack | solution.py:313
  3.5 0.0 copy-done
  3.5 0.0 copy-done.5
  3.5 0.7 %select_convert_fusion.lab_ref = f32[128,128]{1,0:T(8,128)} fusion(s32[128,128]{1,0:T(8,128)S(1)} %copy-done, s32[128]{0:T(128)S(1)} %copy-done.5), kind=kLoop, calls=%fused_computation | loop fusion | flops 49152 | bytes 131584 | tf_op jit(solution)/shard_map/convert_element_type | solution.py:312
  4.3 33.1 %shard_map.129 = (f32[16,512]{1,0:T(8,128)}, f32[16,512]{1,0:T(8,128)}, f32[16,512]{1,0:T(8,128)}, f32[16,16]{1,0:T(8,128)}) custom-call(bf16[32,128,128]{2,1,0:T(8,128)(2,1)} %bitcast.3, f32[128,128]{1,0:T(8,128)} %select_convert_fusion.lab_ref, s32[1,128]{1,0:T(1,128)} %bitcast.5, f32[16,512]{1,0:T(8,128)} %pos_ref.1, f32[16,512]{1,0:T(8,128)} %mom_ref.1, ...), custom_call_target="tpu_custom_call" | custom-call | tf_op jit(solution)/shard_map/pallas_call | solution.py:318
  37.4 0.0 copy-start.2
  37.4 1.4 %copy.18 = f32[16,512]{1,0:T(8,128)} copy(f32[16,512]{1,0:T(8,128)} %get-tuple-element.8) | data formatting | bytes 65536
  38.8 0.0 copy-done.2
  38.8 0.0 copy-start.1
  38.8 0.6 %copy.19 = f32[16,512]{1,0:T(8,128)} copy(f32[16,512]{1,0:T(8,128)S(1)} %copy-done.2) | data formatting | bytes 65536
  39.4 0.2 copy-done.1
  39.5 0.0 copy-start.3
  39.5 0.6 %copy.20 = f32[16,512]{1,0:T(8,128)} copy(f32[16,512]{1,0:T(8,128)S(1)} %copy-done.1) | data formatting | bytes 65536
  40.2 0.1 copy-done.3
  40.2 0.6 %copy.21 = f32[16,16]{1,0:T(8,128)} copy(f32[16,16]{1,0:T(8,128)S(1)} %copy-done.3) | data formatting | bytes 2048
Async XLA Ops:
  0.6 2.9 %copy-start = (s32[128,128]{1,0:T(8,128)S(1)}, s32[128,128]{1,0:T(8,128)}, u32[]{:S(2)}) copy-start(s32[128,128]{1,0:T(8,128)} %param.11) | copy-start | bytes 196612
  2.2 0.7 %copy-start.4 = (f32[512]{0:T(512)S(1)}, f32[512]{0:T(512)}, u32[]{:S(2)}) copy-start(f32[512]{0:T(512)} %param.17) | copy-start | bytes 6148
  2.9 0.7 %copy-start.5 = (s32[128]{0:T(128)S(1)}, s32[128]{0:T(128)}, u32[]{:S(2)}) copy-start(s32[128]{0:T(128)} %param.12) | copy-start | bytes 1540
  37.4 1.4 %copy-start.2 = (f32[16,512]{1,0:T(8,128)S(1)}, f32[16,512]{1,0:T(8,128)}, u32[]{:S(2)}) copy-start(f32[16,512]{1,0:T(8,128)} %get-tuple-element.9) | copy-start | bytes 98308
  38.8 0.8 %copy-start.1 = (f32[16,512]{1,0:T(8,128)S(1)}, f32[16,512]{1,0:T(8,128)}, u32[]{:S(2)}) copy-start(f32[16,512]{1,0:T(8,128)} %get-tuple-element.10) | copy-start | bytes 98308
  39.5 0.7 %copy-start.3 = (f32[16,16]{1,0:T(8,128)S(1)}, f32[16,16]{1,0:T(8,128)}, u32[]{:S(2)}) copy-start(f32[16,16]{1,0:T(8,128)} %get-tuple-element.11) | copy-start | bytes 3076

commit v2 on v1

--- a/solution.py
+++ b/solution.py
@@ -8,7 +8,7 @@
 
 step_size = 0.1
 LANES = 128
-CHUNKS = 4
+CHUNKS = 8
 MESH = pl.DeviceIdType.MESH
 BF16 = jnp.bfloat16
 F32 = jnp.float32
@@ -29,11 +29,12 @@
 
 def kernel(
     n, nf, chains, quarter,
-    obs_hbm, lab_ref, grp_ref, pos_ref, mom_ref, grad_ref, par_ref,
-    newpos_ref, newmom_ref, newgrad_ref, energy_ref,
-    obs, perm, wsrc, wall, half_ref, lhs, mine, pair_send, pair_recv,
-    far_send, far_recv, res_own, res_recv, nll_ref, dmat, gsend, grecv, esend, erecv,
-    obs_sem, w_ssem, w_rsem, p_ssem, p_rsem, f_ssem, f_rsem, r_ssem, r_rsem,
+    obs_hbm, lab_hbm, live_hbm, grp_hbm, pos_hbm, mom_hbm, grad_hbm, mean_hbm, prec_hbm, mass_hbm,
+    newpos_out, newmom_out, newgrad_out, energy_out,
+    lab_in, live_ref, grp_ref, pos_ref, mom_ref, grad_ref, mean_ref, pair_ref,
+    lab_ref, par_ref, newpos_ref, newmom_ref, newgrad_ref, energy_ref, obs, perm, wsrc, wall, half_ref, lhs, mine, pair_send, pair_recv,
+    far_send, far_recv, res_own, res_recv, nll_ref, dmat, gsend0, gsend1, grecv0, grecv1, esend, erecv,
+    in_sem, out_sem, w_ssem, w_rsem, p_ssem, p_rsem, f_ssem, f_rsem, r_ssem, r_rsem,
     g_ssem, g_rsem, e_ssem, e_rsem,
 ):
     me = lax.axis_index("dp")
@@ -52,8 +53,6 @@
     near = feat + 1 - 2 * bit
     far = (feat + nf // 2) % nf
 
-    fetch = pltpu.make_async_copy(obs_hbm, obs, obs_sem)
-    fetch.start()
     barrier = pltpu.get_barrier_semaphore()
 
     def greet(i, carry):
@@ -64,18 +63,40 @@
     for i in range(1, nf):
         pl.semaphore_signal(barrier, inc=1, device_id={"feat": (feat + i) % nf}, device_id_type=MESH)
 
+    sources = [
+        (pos_hbm, pos_ref), (mom_hbm, mom_ref), (grad_hbm, grad_ref), (mean_hbm, mean_ref),
+        (prec_hbm, pair_ref.at[0:1]), (mass_hbm, pair_ref.at[1:2]), (grp_hbm, grp_ref),
+        (live_hbm, live_ref), (lab_hbm, lab_in), (obs_hbm, obs),
+    ]
+    fetches = [pltpu.make_async_copy(a, b, in_sem.at[i]) for i, (a, b) in enumerate(sources)]
+    for f in fetches:
+        f.start()
+    spread = (iota((quarter, width), 0) == iota((quarter, width), 1) // chains).astype(F32)
     r, c = iota((width, width), 0), iota((width, width), 1)
     perm[...] = jnp.where(
         (r % chains == c // quarter) & (r // chains == c % quarter), 1.0, 0.0
     ).astype(BF16)
+    for f in fetches[:-1]:
+        f.wait()
+    par_ref[...] = jnp.dot(
+        pair_ref[...], spread, precision=lax.Precision.HIGHEST, preferred_element_type=F32
+    )
     half = mom_ref[...] - 0.5 * step_size * grad_ref[...]
     half_ref[...] = half
-    moved = pos_ref[...] + step_size * par_ref[2:3, :] * half
+    moved = pos_ref[...] + step_size * par_ref[1:2, :] * half
     newpos_ref[...] = moved
+    out_pos = pltpu.make_async_copy(newpos_ref, newpos_out, out_sem.at[0])
+    out_pos.start()
     coeff = jnp.dot(moved.astype(BF16), perm[...], preferred_element_type=F32).astype(BF16)
     wsrc[...] = coeff
     own_rows = pl.ds(pl.multiple_of(me * own, own), own)
     wall[own_rows, :] = coeff
+    square = iota((tiles, tiles), 0) == iota((tiles, tiles), 1)
+    live_col = jnp.sum(jnp.where(square, live_ref[...].astype(F32), 0.0), axis=1, keepdims=True)
+    lab_ref[...] = jnp.where(
+        iota(lab_ref.shape, 1).astype(F32) < live_col, lab_in[...].astype(F32), -1.0
+    )
+    nll_ref[...] = jnp.zeros_like(nll_ref)
     pl.semaphore_wait(barrier, n - 1 + nf - 1)
 
     def w_copy(i):
@@ -112,7 +133,7 @@
             for s in range(1, pack):
                 y = jnp.where((place + pack - j) % pack == s, turned[s], y)
             lhs[pl.ds(m * pack + j, tiles, stride=chains), :] = jnp.where(keep, y, 0.0)
-    fetch.wait()
+    fetches[-1].wait()
 
     def logits(first_quad, dst, base):
         for i in range(chunk_quads):
@@ -152,7 +173,6 @@
         logits(bit * half_quads + k * chunk_quads, mine, k * crows)
         return carry
 
-    lax.fori_loop(0, CHUNKS, stage_a, 0)
 
     def stage_b(k, carry):
         pair_copy(k).wait()
@@ -162,9 +182,15 @@
         far_copy(k).start()
         return carry
 
-    lax.fori_loop(0, CHUNKS, stage_b, 0)
-
-    nll_ref[...] = jnp.zeros_like(nll_ref)
+    def stage_ab(k, carry):
+        stage_a(k, 0)
+        stage_b(k - 1, 0)
+        return carry
+
+    stage_a(0, 0)
+    lax.fori_loop(1, CHUNKS, stage_ab, 0)
+    stage_b(CHUNKS - 1, 0)
+
     diag = iota((qrows, LANES), 0) // chains == iota((qrows, LANES), 1) // quarter
 
     def grads(first_quad, src, k):
@@ -205,17 +231,20 @@
     lax.fori_loop(0, CHUNKS, stage_d, 0)
 
     lane_g = iota((seg_groups, LANES), 1) // quarter
-
-    def segment(gc, carry):
+    count = width // LANES
+    cut = count // 2
+    sums = ((gsend0, grecv0, range(cut), True), (gsend1, grecv1, range(cut, count), False))
+
+    def stacked(d):
+        return jnp.concatenate(split(d), axis=0)
+
+    def segment(gc, part):
+        gsend, _, blocks, with_nll = sums[part]
         base = gc * seg_groups
         out = pl.ds(pl.multiple_of(base, seg_groups), seg_groups)
         oh = (iota((seg_groups, tiles), 0) + base == grp_ref[...]).astype(F32).astype(BF16)
         oh = jnp.concatenate([oh, oh], axis=1)
-
-        def stacked(d):
-            return jnp.concatenate(split(d), axis=0)
-
-        for m in range(width // LANES):
+        for b, m in enumerate(blocks):
             packed = None
             for j in range(0, pack, 2):
                 at = (m * pack + j) * tiles
@@ -230,49 +259,61 @@
                         s = s + pltpu.roll(s, shift, 1)
                         shift //= 2
                     packed = s if packed is None else jnp.where(lane_g == j + h, s, packed)
-            gsend[out, m * LANES:(m + 1) * LANES] = packed.astype(BF16)
-        hi, lo = split(jnp.dot(oh, stacked(nll_ref[...]), preferred_element_type=F32))
-        gsend[out, width:width + LANES] = (
-            hi.astype(F32) + pltpu.roll(lo.astype(F32), chains, 1)
-        ).astype(BF16)
-        return carry
-
-    lax.fori_loop(0, groups // seg_groups, segment, 0)
-
-    def g_copy(i):
+            gsend[out, b * LANES:(b + 1) * LANES] = packed.astype(BF16)
+        if with_nll:
+            hi, lo = split(jnp.dot(oh, stacked(nll_ref[...]), preferred_element_type=F32))
+            gsend[out, len(blocks) * LANES:] = (
+                hi.astype(F32) + pltpu.roll(lo.astype(F32), chains, 1)
+            ).astype(BF16)
+
+    def g_copy(part, i):
         to = (me + i) % n
         return pltpu.make_async_remote_copy(
-            src_ref=gsend.at[pl.ds(pl.multiple_of(to * own, own), own)],
-            dst_ref=grecv.at[me], send_sem=g_ssem.at[i], recv_sem=g_rsem.at[i],
+            src_ref=sums[part][0].at[pl.ds(pl.multiple_of(to * own, own), own)],
+            dst_ref=sums[part][1].at[me], send_sem=g_ssem.at[part, i], recv_sem=g_rsem.at[part, i],
             device_id={"dp": to}, device_id_type=MESH,
         )
 
-    def start_g(i, carry):
-        g_copy(i).start()
-        return carry
-
-    lax.fori_loop(1, n, start_g, 0)
-    grecv[me] = gsend[own_rows, :]
+    for part in range(2):
+        def run(gc, carry, part=part):
+            segment(gc, part)
+            return carry
+
+        def start_g(i, carry, part=part):
+            g_copy(part, i).start()
+            return carry
+
+        lax.fori_loop(0, groups // seg_groups, run, 0)
+        lax.fori_loop(1, n, start_g, 0)
+        sums[part][1][me] = sums[part][0][own_rows, :]
 
     def wait_g(i, carry):
-        g_copy(i).wait()
+        g_copy(0, i).wait()
+        g_copy(1, i).wait()
         return carry
 
     lax.fori_loop(1, n, wait_g, 0)
 
     def add_g(i, total):
-        return total + grecv[i].astype(F32)
-
-    total = lax.fori_loop(0, n, add_g, jnp.zeros((own, width + LANES), F32))
-    parts = jnp.concatenate(split(total[:, :width]), axis=0)
+        return total[0] + grecv0[i].astype(F32), total[1] + grecv1[i].astype(F32)
+
+    first, second = lax.fori_loop(0, n, add_g, (
+        jnp.zeros((own, (cut + 1) * LANES), F32), jnp.zeros((own, (count - cut) * LANES), F32)
+    ))
+    lik_packed = jnp.concatenate([first[:, :cut * LANES], second], axis=1)
+    parts = jnp.concatenate(split(lik_packed), axis=0)
     natural = nt_dot(parts, perm[...])
     lik = natural[:own] + natural[own:]
-    mean, prec, mass = par_ref[0:1, :], par_ref[1:2, :], par_ref[2:3, :]
+    mean, prec, mass = mean_ref[...], par_ref[0:1, :], par_ref[1:2, :]
     offset = newpos_ref[...] - mean
     new_gradient = lik + prec * offset
     new_momentum = half_ref[...] - 0.5 * step_size * new_gradient
     newgrad_ref[...] = new_gradient
     newmom_ref[...] = new_momentum
+    out_grad = pltpu.make_async_copy(newgrad_ref, newgrad_out, out_sem.at[1])
+    out_mom = pltpu.make_async_copy(newmom_ref, newmom_out, out_sem.at[2])
+    out_grad.start()
+    out_mom.start()
     quad = 0.5 * (prec * offset * offset + mass * new_momentum * new_momentum)
     q = quad[:, :LANES]
     for m in range(1, width // LANES):
@@ -281,7 +322,7 @@
     while shift >= chains:
         q = q + pltpu.roll(q, shift, 1)
         shift //= 2
-    loss = total[:, width:]
+    loss = first[:, cut * LANES:]
     loss = loss + pltpu.roll(loss, LANES - chains, 1)
     esend[...] = q + loss
 
@@ -300,6 +341,15 @@
     for i in range(1, nf):
         e = e + erecv[i]
     energy_ref[...] = e[:, :chains]
+    out_energy = pltpu.make_async_copy(energy_ref, energy_out, out_sem.at[3])
+    out_energy.start()
+    for f in (out_pos, out_grad, out_mom, out_energy):
+        f.wait()
+
+
+def finish(*refs):
+    for a, b in zip(refs[:4], refs[4:]):
+        b[...] = a[...]
 
 
 def body(observations, labels, tile_live, tile_group, position, momentum, gradient, prior_mean, prior_prec, inv_mass):
@@ -308,19 +358,31 @@
     own, width = position.shape
     chains = width // quarter
     pack = LANES // quarter
-    alive = jnp.arange(row_count, dtype=jnp.int32)[None, :] < tile_live[:, None]
-    marked = jnp.where(alive, labels, -1).astype(F32)
-    par = jnp.stack([prior_mean, jnp.repeat(prior_prec, chains), jnp.repeat(inv_mass, chains)])
     half_rows = tiles * chains // 2
-    vmem = pl.BlockSpec(memory_space=pltpu.VMEM)
+    anywhere = pl.BlockSpec(memory_space=pl.ANY)
+    cut = width // LANES // 2 * LANES
     dma = pltpu.SemaphoreType.DMA
     block = jax.ShapeDtypeStruct((own, width), F32)
-    return tuple(pl.pallas_call(
+    results = pl.pallas_call(
         functools.partial(kernel, n, nf, chains, quarter),
         out_shape=(block, block, block, jax.ShapeDtypeStruct((own, chains), F32)),
-        in_specs=[pl.BlockSpec(memory_space=pl.ANY)] + [vmem] * 6,
-        out_specs=(vmem,) * 4,
+        in_specs=[anywhere] * 10,
+        out_specs=(anywhere,) * 4,
         scratch_shapes=[
+            pltpu.VMEM((tiles, row_count), jnp.int32),
+            pltpu.VMEM((1, tiles), jnp.int32),
+            pltpu.VMEM((1, tiles), jnp.int32),
+            pltpu.VMEM((own, width), F32),
+            pltpu.VMEM((own, width), F32),
+            pltpu.VMEM((own, width), F32),
+            pltpu.VMEM((1, width), F32),
+            pltpu.VMEM((2, quarter), F32),
+            pltpu.VMEM((tiles, row_count), F32),
+            pltpu.VMEM((2, width), F32),
+            pltpu.VMEM((own, width), F32),
+            pltpu.VMEM((own, width), F32),
+            pltpu.VMEM((own, width), F32),
+            pltpu.VMEM((own, chains), F32),
             pltpu.VMEM((tiles // pack, LANES, row_count), BF16),
             pltpu.VMEM((width, width), BF16),
             pltpu.VMEM((own, width), BF16),
@@ -336,25 +398,33 @@
             pltpu.VMEM((half_rows, row_count), BF16),
             pltpu.VMEM((tiles, LANES), F32),
             pltpu.VMEM((chains * tiles, LANES), F32),
-            pltpu.VMEM((n * own, width + LANES), BF16),
-            pltpu.VMEM((n, own, width + LANES), BF16),
+            pltpu.VMEM((n * own, cut + LANES), BF16),
+            pltpu.VMEM((n * own, width - cut), BF16),
+            pltpu.VMEM((n, own, cut + LANES), BF16),
+            pltpu.VMEM((n, own, width - cut), BF16),
             pltpu.VMEM((own, LANES), F32),
             pltpu.VMEM((nf, own, LANES), F32),
-            dma,
+            dma((10,)), dma((4,)),
             dma((n,)), dma((n,)),
             dma((CHUNKS,)), dma((CHUNKS,)),
             dma((CHUNKS,)), dma((CHUNKS,)),
             dma((CHUNKS,)), dma((CHUNKS,)),
-            dma((n,)), dma((n,)),
+            dma((2, n)), dma((2, n)),
             dma((nf,)), dma((nf,)),
         ],
         compiler_params=pltpu.CompilerParams(collective_id=0, has_side_effects=True),
     )(
         observations.reshape(tiles // pack, LANES, row_count),
-        marked,
-        tile_group.reshape(1, tiles),
-        position, momentum, gradient, par,
-    ))
+        labels, tile_live.reshape(1, tiles), tile_group.reshape(1, tiles),
+        position, momentum, gradient,
+        prior_mean.reshape(1, width), prior_prec.reshape(1, quarter), inv_mass.reshape(1, quarter),
+    )
+    return tuple(pl.pallas_call(
+        finish,
+        out_shape=tuple(jax.ShapeDtypeStruct(x.shape, x.dtype) for x in results),
+        in_specs=[pl.BlockSpec(memory_space=pltpu.VMEM)] * 4,
+        out_specs=(pl.BlockSpec(memory_space=pltpu.VMEM),) * 4,
+    )(*results))
 
 
 def solution(mesh):

time: 41.3 us -> 35.5 us (0.86)
  local copies, waits for them, and re-layouts: 5.76 us -> 0 us
  Pallas kernels: 33.1 us -> 34.6 us
  other arithmetic: 1.32 us -> 0 us
    unnamed x16 -> x0, local copies, waits for them, and re-layouts: 4.11 us -> none
    broadcast_in_dim x2 -> x0, local copies, waits for them, and re-layouts: 1.48 us -> none  [the longest x1 0.76 us: body(): jnp.repeat(prior_prec, chains)]
    pallas_call x0 -> x1, Pallas kernels: none -> 1.44 us  [body(): pl.pallas_call(finish, out_shape=tuple((jax.ShapeDtypeStruct(x.shape, x.d...]
    convert_element_type x1 -> x0, other arithmetic: 0.71 us -> none  [body(): marked = jnp.where(alive, labels, -1).astype(F32)]
    another operation x1 -> x0, other arithmetic: 0.61 us -> none  [body(): jnp.stack([prior_mean, jnp.repeat(prior_prec, chains), jnp.repeat(inv_mas...]
where the time goes in v2:
time: 35.5 us; the launch traced here: 35.3 us
  Pallas kernels  34.6 us (97%)
  between operations  0.64 us (2%)
    pallas_call x1, Pallas kernels, body(): pl.pallas_call(functools.partial(kernel, n, nf, chains, quarter), out_sha...  33.2 us
    pallas_call x1, Pallas kernels, body(): pl.pallas_call(finish, out_shape=tuple((jax.ShapeDtypeStruct(x.shape, x.d...  1.44 us

profile of v2, /device:TPU:0, one launch (start us, length us, event | category | flops | bytes accessed | tf_op | source)
XLA Modules:
  0.0 35.3 jit_solution(3239636204944900163)
XLA Ops:
  0.6 33.2 %shard_map.129 = (f32[16,512]{1,0:T(8,128)}, f32[16,512]{1,0:T(8,128)}, f32[16,512]{1,0:T(8,128)}, f32[16,16]{1,0:T(8,128)}) custom-call(bf16[32,128,128]{2,1,0:T(8,128)(2,1)} %bitcast.6, s32[128,128]{1,0:T(8,128)} %lab_hbm.1, s32[1,128]{1,0:T(1,128)} %bitcast.8, s32[1,128]{1,0:T(1,128)} %bitcast.9, f32[16,512]{1,0:T(8,128)} %pos_hbm.1, f32[16,512]{1,0:T(8,128)} %mom_hbm.1, ...), custom_call_target="tpu_custom_call" | custom-call | tf_op jit(solution)/shard_map/pallas_call | solution.py:366
  33.8 1.4 %shard_map.130 = (f32[16,512]{1,0:T(8,128)}, f32[16,512]{1,0:T(8,128)}, f32[16,512]{1,0:T(8,128)}, f32[16,16]{1,0:T(8,128)}) custom-call(f32[16,512]{1,0:T(8,128)} %get-tuple-element.8.refs_0_, f32[16,512]{1,0:T(8,128)} %get-tuple-element.9.refs_1_, f32[16,512]{1,0:T(8,128)} %get-tuple-element.10.refs_2_, f32[16,16]{1,0:T(8,128)} %get-tuple-element.11.refs_3_), custom_call_target="tpu_custom_call" | custom-call | tf_op jit(solution)/shard_map/pallas_call | solution.py:422
